TPU v7x, 32 devices: a whole 2x2x4 slice. The times are simulated.
32 devices in a mesh: dp: 4 (over y, x), fsdp: 8 (over z, core).
Axes of the slice: x: 2, y: 2, z: 4, core: 2. Of those that a mesh axis runs over, the one named last changes fastest.
Arguments:
- tokens: bfloat16 [32, 1024, 768], P(('dp', 'fsdp')), may hold values from -6 to 6
- lengths: int32 [32], P(('dp', 'fsdp')), may hold values from 256 to 1024, as said below
- cells: int32 [32, 1024], P(('dp', 'fsdp')), may hold values 0 or 1
- cotangent: bfloat16 [32, 1024, 768], P(('dp', 'fsdp')), may hold values from -6 to 6
- ln1_gain: bfloat16 [768], P('fsdp'), may hold values from 0.5 to 1.5
- ln1_bias: bfloat16 [768], P('fsdp'), may hold values from -3 to 3
- w_qkv: bfloat16 [768, 2304], P('fsdp'), may hold values from -0.21875 to 0.21875
- b_query: bfloat16 [768], P('fsdp'), may hold values from -6 to 6
- b_value: bfloat16 [768], P('fsdp'), may hold values from -6 to 6
- w_out: bfloat16 [768, 768], P('fsdp'), may hold values from -0.875 to 0.875
- b_out: bfloat16 [768], P('fsdp'), may hold values from -3 to 3
- ln2_gain: bfloat16 [768], P('fsdp'), may hold values from 0.5 to 1.5
- ln2_bias: bfloat16 [768], P('fsdp'), may hold values from -3 to 3
- w_up: bfloat16 [768, 3072], P('fsdp'), may hold values from -0.21875 to 0.21875
- b_up: bfloat16 [3072], P('fsdp'), may hold values from -3 to 3
- w_down: bfloat16 [3072, 768], P('fsdp'), may hold values from -0.109375 to 0.109375
- b_down: bfloat16 [768], P('fsdp'), may hold values from -3 to 3
Outputs:
- output: bfloat16 [32, 1024, 768], P(('dp', 'fsdp'))
- grad_tokens: float32 [32, 1024, 768], P(('dp', 'fsdp'))
- grad_ln1_gain: float32 [768], P('fsdp')
- grad_ln1_bias: float32 [768], P('fsdp')
- grad_w_qkv: float32 [768, 2304], P('fsdp')
- grad_b_query: float32 [768], P('fsdp')
- grad_b_value: float32 [768], P('fsdp')
- grad_w_out: float32 [768, 768], P('fsdp')
- grad_b_out: float32 [768], P('fsdp')
- grad_ln2_gain: float32 [768], P('fsdp')
- grad_ln2_bias: float32 [768], P('fsdp')
- grad_w_up: float32 [768, 3072], P('fsdp')
- grad_b_up: float32 [3072], P('fsdp')
- grad_w_down: float32 [3072, 768], P('fsdp')
- grad_b_down: float32 [768], P('fsdp')
Inputs may be any that keep to these rules, and one draw needn't show every extreme that they name: `lengths`: each sequence has at least 256 valid tokens, and some sequence fills all 1024 slots.
All inputs are finite; a program needn't handle non-finite values. No bound on the sum of `cells` on one device may be relied on, other than what follows from the above.
Results may differ from a plain program's by a relative error of at most 0.019.
Values may be sent and summed in bfloat16 or wider, within the bound.
A program may use at most 128 MiB of HBM per device.

v0:
```python
from functools import partial
import math
import jax
import jax.numpy as jnp
from jax import lax
from jax.sharding import PartitionSpec as P

H = 12
EPSILON = 1e-05
GELU_C = 0.7978845608028654
GELU_A = 0.044715


def norm_forward(values):
    row_mean = jnp.mean(values, axis=-1, keepdims=True)
    centered = values - row_mean
    inv_std = lax.rsqrt(jnp.mean(centered * centered, axis=-1, keepdims=True) + EPSILON)
    return (centered * inv_std, inv_std)


def norm_backward(grad_normed, normalized, inv_std, gain):
    scaled = grad_normed * gain
    return inv_std * (
        scaled
        - jnp.mean(scaled, axis=-1, keepdims=True)
        - normalized * jnp.mean(scaled * normalized, axis=-1, keepdims=True)
    )


def gelu_pair(values):
    cubic = values * values * values
    tanh_part = jnp.tanh(GELU_C * (values + GELU_A * cubic))
    result = 0.5 * values * (1.0 + tanh_part)
    slope = 0.5 * (1.0 + tanh_part) + 0.5 * values * (1.0 - tanh_part * tanh_part) * GELU_C * (
        1.0 + 3.0 * GELU_A * values * values
    )
    return (result, slope)


def allowed_blocks(lengths, cells, context):
    positions = jnp.arange(context)
    query_pos = positions[None, :, None]
    key_pos = positions[None, None, :]
    usable = (key_pos <= query_pos) & (key_pos < lengths[:, None, None]) & (cells[:, None, :] == 1)
    return usable | (key_pos == query_pos)


def split_heads(rows, seqs, context, heads):
    width = rows.shape[1]
    return rows.reshape(seqs, context, heads, width // heads).transpose(2, 0, 1, 3)


def join_heads(stacked):
    return stacked.transpose(1, 2, 0, 3).reshape(-1, stacked.shape[0] * stacked.shape[3])


def head_forward(allowed, operands):
    query_head, key_head, value_head = operands
    scores = jnp.einsum("sqd,skd->sqk", query_head, key_head, preferred_element_type=jnp.float32)
    scores = jnp.where(allowed, scores, -1e30)
    row_max = jnp.max(scores, axis=-1, keepdims=True)
    exponent = jnp.exp(scores - row_max)
    row_total = jnp.sum(exponent, axis=-1, keepdims=True)
    softmax_rows = (exponent / row_total).astype(jnp.bfloat16)
    attended = jnp.einsum(
        "sqk,skd->sqd", softmax_rows, value_head, preferred_element_type=jnp.float32
    )
    return (attended, (row_max + jnp.log(row_total))[..., 0])


def head_backward(allowed, operands):
    query_head, key_head, value_head, grad_head, log_total = operands
    scores = jnp.einsum("sqd,skd->sqk", query_head, key_head, preferred_element_type=jnp.float32)
    softmax_rows = jnp.where(allowed, jnp.exp(scores - log_total[..., None]), 0.0)
    grad_values = jnp.einsum(
        "sqk,sqd->skd",
        softmax_rows.astype(jnp.bfloat16),
        grad_head,
        preferred_element_type=jnp.float32,
    )
    grad_probs = jnp.einsum(
        "sqd,skd->sqk", grad_head, value_head, preferred_element_type=jnp.float32
    )
    inner = jnp.sum(softmax_rows * grad_probs, axis=-1, keepdims=True)
    grad_scores = (softmax_rows * (grad_probs - inner)).astype(jnp.bfloat16)
    grad_queries = jnp.einsum(
        "sqk,skd->sqd", grad_scores, key_head, preferred_element_type=jnp.float32
    )
    grad_keys = jnp.einsum(
        "sqk,sqd->skd", grad_scores, query_head, preferred_element_type=jnp.float32
    )
    return (grad_queries, grad_keys, grad_values)


def per_device(
    tokens,
    lengths,
    cells,
    cotangent,
    ln1_gain,
    ln1_bias,
    w_qkv,
    b_query,
    b_value,
    w_out,
    b_out,
    ln2_gain,
    ln2_bias,
    w_up,
    b_up,
    w_down,
    b_down,
):
    seqs, context, width = tokens.shape
    heads = H
    scale = 1.0 / math.sqrt(width // heads)
    attn_parts = (
        lax.all_gather(ln1_gain, "fsdp", axis=0, tiled=True),
        lax.all_gather(ln1_bias, "fsdp", axis=0, tiled=True),
        lax.all_gather(w_qkv, "fsdp", axis=0, tiled=True),
        lax.all_gather(b_query, "fsdp", axis=0, tiled=True),
        lax.all_gather(b_value, "fsdp", axis=0, tiled=True),
        lax.all_gather(w_out, "fsdp", axis=0, tiled=True),
        lax.all_gather(b_out, "fsdp", axis=0, tiled=True),
    )
    gain_one, shift_one, qkv_full, bias_query, bias_value, out_full, bias_out = attn_parts
    inputs = tokens.reshape(-1, width).astype(jnp.float32)
    normal_one, inv_one = norm_forward(inputs)
    normed_one = (normal_one * gain_one.astype(jnp.float32) + shift_one.astype(jnp.float32)).astype(
        jnp.bfloat16
    )
    projected = jnp.dot(normed_one, qkv_full, preferred_element_type=jnp.float32)
    queries = ((projected[:, :width] + bias_query.astype(jnp.float32)) * scale).astype(jnp.bfloat16)
    key_rows = projected[:, width : 2 * width].astype(jnp.bfloat16)
    value_rows = (projected[:, 2 * width :] + bias_value.astype(jnp.float32)).astype(jnp.bfloat16)
    allowed = allowed_blocks(lengths, cells, context)
    query_heads = split_heads(queries, seqs, context, heads)
    key_heads = split_heads(key_rows, seqs, context, heads)
    value_heads = split_heads(value_rows, seqs, context, heads)
    attended_heads, log_totals = lax.map(
        partial(head_forward, allowed), (query_heads, key_heads, value_heads)
    )
    attended = join_heads(attended_heads).astype(jnp.bfloat16)
    middle = (
        inputs
        + jnp.dot(attended, out_full, preferred_element_type=jnp.float32)
        + bias_out.astype(jnp.float32)
    )
    mlp_parts = (
        lax.all_gather(ln2_gain, "fsdp", axis=0, tiled=True),
        lax.all_gather(ln2_bias, "fsdp", axis=0, tiled=True),
        lax.all_gather(w_up, "fsdp", axis=0, tiled=True),
        lax.all_gather(b_up, "fsdp", axis=0, tiled=True),
        lax.all_gather(w_down, "fsdp", axis=0, tiled=True),
        lax.all_gather(b_down, "fsdp", axis=0, tiled=True),
    )
    gain_two, shift_two, up_full, bias_up, down_full, bias_down = mlp_parts
    normal_two, inv_two = norm_forward(middle)
    normed_two = (normal_two * gain_two.astype(jnp.float32) + shift_two.astype(jnp.float32)).astype(
        jnp.bfloat16
    )
    hidden_pre = jnp.dot(normed_two, up_full, preferred_element_type=jnp.float32) + bias_up.astype(
        jnp.float32
    )
    activated, slope = gelu_pair(hidden_pre)
    activated = activated.astype(jnp.bfloat16)
    mlp_out = jnp.dot(activated, down_full, preferred_element_type=jnp.float32) + bias_down.astype(
        jnp.float32
    )
    result = (middle + mlp_out).astype(jnp.bfloat16).reshape(tokens.shape)
    valid = (jnp.arange(context)[None, :] < lengths[:, None]).astype(jnp.float32).reshape(-1, 1)
    grad_out = cotangent.reshape(-1, width).astype(jnp.float32) * valid
    mlp_back = (
        lax.all_gather(ln2_gain, "fsdp", axis=0, tiled=True),
        lax.all_gather(ln2_bias, "fsdp", axis=0, tiled=True),
        lax.all_gather(w_up, "fsdp", axis=0, tiled=True),
        lax.all_gather(b_up, "fsdp", axis=0, tiled=True),
        lax.all_gather(w_down, "fsdp", axis=0, tiled=True),
        lax.all_gather(b_down, "fsdp", axis=0, tiled=True),
    )
    gain_two_back, unused_two, up_back, unused_up, down_back, unused_down = mlp_back
    grad_mlp = grad_out.astype(jnp.bfloat16)
    grad_down = jnp.einsum("rf,rd->fd", activated, grad_mlp, preferred_element_type=jnp.float32)
    grad_bias_down = jnp.sum(grad_mlp.astype(jnp.float32), axis=0)
    grad_act = jnp.einsum("rd,fd->rf", grad_mlp, down_back, preferred_element_type=jnp.float32)
    grad_hidden = (grad_act * slope).astype(jnp.bfloat16)
    grad_up = jnp.einsum("rd,rf->df", normed_two, grad_hidden, preferred_element_type=jnp.float32)
    grad_bias_up = jnp.sum(grad_hidden.astype(jnp.float32), axis=0)
    grad_normed_two = jnp.einsum(
        "rf,df->rd", grad_hidden, up_back, preferred_element_type=jnp.float32
    )
    grad_gain_two = jnp.sum(grad_normed_two * normal_two, axis=0)
    grad_shift_two = jnp.sum(grad_normed_two, axis=0)
    grad_middle = grad_out + norm_backward(
        grad_normed_two, normal_two, inv_two, gain_two_back.astype(jnp.float32)
    )
    mlp_rows = (
        lax.psum_scatter(
            grad_gain_two.astype(jnp.bfloat16), "fsdp", scatter_dimension=0, tiled=True
        ).astype(jnp.float32),
        lax.psum_scatter(
            grad_shift_two.astype(jnp.bfloat16), "fsdp", scatter_dimension=0, tiled=True
        ).astype(jnp.float32),
        lax.psum_scatter(
            grad_up.astype(jnp.bfloat16), "fsdp", scatter_dimension=0, tiled=True
        ).astype(jnp.float32),
        lax.psum_scatter(
            grad_bias_up.astype(jnp.bfloat16), "fsdp", scatter_dimension=0, tiled=True
        ).astype(jnp.float32),
        lax.psum_scatter(
            grad_down.astype(jnp.bfloat16), "fsdp", scatter_dimension=0, tiled=True
        ).astype(jnp.float32),
        lax.psum_scatter(
            grad_bias_down.astype(jnp.bfloat16), "fsdp", scatter_dimension=0, tiled=True
        ).astype(jnp.float32),
    )
    row_gain_two, row_shift_two, row_up, row_bias_up, row_down, row_bias_down = mlp_rows
    mlp_sums = (
        lax.psum(row_gain_two.astype(jnp.bfloat16), "dp").astype(jnp.float32),
        lax.psum(row_shift_two.astype(jnp.bfloat16), "dp").astype(jnp.float32),
        lax.psum(row_up.astype(jnp.bfloat16), "dp").astype(jnp.float32),
        lax.psum(row_bias_up.astype(jnp.bfloat16), "dp").astype(jnp.float32),
        lax.psum(row_down.astype(jnp.bfloat16), "dp").astype(jnp.float32),
        lax.psum(row_bias_down.astype(jnp.bfloat16), "dp").astype(jnp.float32),
    )
    attn_back = (
        lax.all_gather(ln1_gain, "fsdp", axis=0, tiled=True),
        lax.all_gather(ln1_bias, "fsdp", axis=0, tiled=True),
        lax.all_gather(w_qkv, "fsdp", axis=0, tiled=True),
        lax.all_gather(b_query, "fsdp", axis=0, tiled=True),
        lax.all_gather(b_value, "fsdp", axis=0, tiled=True),
        lax.all_gather(w_out, "fsdp", axis=0, tiled=True),
        lax.all_gather(b_out, "fsdp", axis=0, tiled=True),
    )
    gain_one_back, unused_shift, qkv_back, unused_query, unused_value, out_back, unused_out = (
        attn_back
    )
    grad_branch = grad_middle.astype(jnp.bfloat16)
    grad_out_proj = jnp.einsum(
        "rd,re->de", attended, grad_branch, preferred_element_type=jnp.float32
    )
    grad_bias_out = jnp.sum(grad_branch.astype(jnp.float32), axis=0)
    grad_attended = jnp.einsum(
        "re,de->rd", grad_branch, out_back, preferred_element_type=jnp.float32
    ).astype(jnp.bfloat16)
    grad_heads = split_heads(grad_attended, seqs, context, heads)
    grad_query_heads, grad_key_heads, grad_value_heads = lax.map(
        partial(head_backward, allowed),
        (query_heads, key_heads, value_heads, grad_heads, log_totals),
    )
    grad_queries = (join_heads(grad_query_heads) * scale).astype(jnp.bfloat16)
    grad_keys = join_heads(grad_key_heads).astype(jnp.bfloat16)
    grad_values = join_heads(grad_value_heads).astype(jnp.bfloat16)
    grad_projected = jnp.concatenate([grad_queries, grad_keys, grad_values], axis=1)
    grad_qkv = jnp.einsum(
        "rd,re->de", normed_one, grad_projected, preferred_element_type=jnp.float32
    )
    grad_bias_query = jnp.sum(grad_queries.astype(jnp.float32), axis=0)
    grad_bias_value = jnp.sum(grad_values.astype(jnp.float32), axis=0)
    grad_normed_one = jnp.einsum(
        "re,de->rd", grad_projected, qkv_back, preferred_element_type=jnp.float32
    )
    grad_gain_one = jnp.sum(grad_normed_one * normal_one, axis=0)
    grad_shift_one = jnp.sum(grad_normed_one, axis=0)
    grad_inputs = grad_middle + norm_backward(
        grad_normed_one, normal_one, inv_one, gain_one_back.astype(jnp.float32)
    )
    attn_rows = (
        lax.psum_scatter(
            grad_gain_one.astype(jnp.bfloat16), "fsdp", scatter_dimension=0, tiled=True
        ).astype(jnp.float32),
        lax.psum_scatter(
            grad_shift_one.astype(jnp.bfloat16), "fsdp", scatter_dimension=0, tiled=True
        ).astype(jnp.float32),
        lax.psum_scatter(
            grad_qkv.astype(jnp.bfloat16), "fsdp", scatter_dimension=0, tiled=True
        ).astype(jnp.float32),
        lax.psum_scatter(
            grad_bias_query.astype(jnp.bfloat16), "fsdp", scatter_dimension=0, tiled=True
        ).astype(jnp.float32),
        lax.psum_scatter(
            grad_bias_value.astype(jnp.bfloat16), "fsdp", scatter_dimension=0, tiled=True
        ).astype(jnp.float32),
        lax.psum_scatter(
            grad_out_proj.astype(jnp.bfloat16), "fsdp", scatter_dimension=0, tiled=True
        ).astype(jnp.float32),
        lax.psum_scatter(
            grad_bias_out.astype(jnp.bfloat16), "fsdp", scatter_dimension=0, tiled=True
        ).astype(jnp.float32),
    )
    row_gain_one, row_shift_one, row_qkv, row_query, row_value, row_out, row_bias_out = attn_rows
    attn_sums = (
        lax.psum(row_gain_one.astype(jnp.bfloat16), "dp").astype(jnp.float32),
        lax.psum(row_shift_one.astype(jnp.bfloat16), "dp").astype(jnp.float32),
        lax.psum(row_qkv.astype(jnp.bfloat16), "dp").astype(jnp.float32),
        lax.psum(row_query.astype(jnp.bfloat16), "dp").astype(jnp.float32),
        lax.psum(row_value.astype(jnp.bfloat16), "dp").astype(jnp.float32),
        lax.psum(row_out.astype(jnp.bfloat16), "dp").astype(jnp.float32),
        lax.psum(row_bias_out.astype(jnp.bfloat16), "dp").astype(jnp.float32),
    )
    return (
        result,
        grad_inputs.reshape(tokens.shape),
        attn_sums[0],
        attn_sums[1],
        attn_sums[2],
        attn_sums[3],
        attn_sums[4],
        attn_sums[5],
        attn_sums[6],
        mlp_sums[0],
        mlp_sums[1],
        mlp_sums[2],
        mlp_sums[3],
        mlp_sums[4],
        mlp_sums[5],
    )


def solution(mesh):
    in_specs = (
        P(("dp", "fsdp"), None, None),
        P(("dp", "fsdp")),
        P(("dp", "fsdp"), None),
        P(("dp", "fsdp"), None, None),
        P("fsdp"),
        P("fsdp"),
        P("fsdp", None),
        P("fsdp"),
        P("fsdp"),
        P("fsdp", None),
        P("fsdp"),
        P("fsdp"),
        P("fsdp"),
        P("fsdp", None),
        P("fsdp"),
        P("fsdp", None),
        P("fsdp"),
    )
    out_specs = (
        P(("dp", "fsdp"), None, None),
        P(("dp", "fsdp"), None, None),
        P("fsdp"),
        P("fsdp"),
        P("fsdp", None),
        P("fsdp"),
        P("fsdp"),
        P("fsdp", None),
        P("fsdp"),
        P("fsdp"),
        P("fsdp"),
        P("fsdp", None),
        P("fsdp"),
        P("fsdp", None),
        P("fsdp"),
    )
    return jax.shard_map(
        per_device, mesh=mesh, in_specs=in_specs, out_specs=out_specs, check_vma=False
    )
```

profile of v0, /device:TPU:0, one launch (start us, length us, event | category | flops | bytes accessed | tf_op | source)
XLA Modules:
  0.0 642.1 jit_solution(9640326640721068901)
XLA Ops:
  14.4 32.5 %all-reduce.18 = (bf16[768]{0:T(1024)(128)(2,1)S(1)}, bf16[768]{0:T(1024)(128)(2,1)S(1)}, bf16[768]{0:T(1024)(128)(2,1)S(1)}, bf16[768]{0:T(1024)(128)(2,1)S(1)}...) all-reduce(bf16[768]{0:T(1024)(128)(2,1)S(1)} %dynamic-update-slice, ...), channel_id=1, replica_groups=mesh['dp'=4,'fsdp'=8] {'fsdp'}, use_global_device_ids=true, to_apply=%add.1 | all-reduce | flops 5376 | bytes 21504
  52.8 12.7 %all-gather = bf16[8,1,384]{2,1,0:T(2,128)(2,1)S(1)} all-gather(bf16[1,1,384]{2,1,0:T(2,128)(2,1)S(1)} %reshape.386), channel_id=1, replica_groups=mesh['dp'=4,'fsdp'=8] {'fsdp'}, dimensions={0}, use_global_device_ids=true | all-gather | bytes 6912 | tf_op jit(solution)/shard_map/all_gather | solution.py:153
  65.7 6.3 fusion.98
  87.1 69.4 %while.30 = (s32[]{:T(128)}, bf16[12,1,1024,64]{2,3,1,0:T(8,128)(2,1)S(1)}, f32[12,1,1024]{2,1,0:T(1,128)S(1)}, bf16[12,1,1024,64]{3,2,1,0:T(8,128)(2,1)}, bf16[...) while((s32[]{:T(128)}, ...), condition=%wide.region_5.6_spmd.clone.clone, body=%wide.region_2.5_spmd.clone.sunk.clone | while | flops 281017344 | bytes 13676633 | solution.py:140
  157.7 3.9 fusion.106
  162.0 10.7 %fusion.100 = f32[1024,3072]{1,0:T(8,128)} fusion(bf16[768,3072]{1,0:T(8,128)(2,1)} %all-gather.10.cloned.1.call-done, f32[1024,768]{0,1:T(8,128)S(1)} %get-tuple-element.332, f32[768]{0:T(1024)S(1)} %convert_element_type.246, f32[768]{0:T(1024)S(1)} %convert_element_type.245, f32[1024]{0:T(1024)S(1)} %add_rsqrt_fusion, f32[1024]{0:T(1024)S(1)} %broadcast_multiply_fusion.4), kind=kOutput, calls=%fused_computation.139 | convolution fusion | flops 4835770368 | bytes 20461568 | tf_op jit(solution)/shard_map/dot_general | solution.py:162
  172.6 9.1 %all-gather.12.cloned.1.call-done = bf16[3072,768]{1,0:T(8,128)(2,1)} async-done(((bf16[384,768]{1,0:T(8,128)(2,1)}), bf16[3072,768]{1,0:T(8,128)(2,1)}) %all-gather.12.cloned.1.call-update) | async-done | bytes 4718608 | tf_op jit(solution)/shard_map/all_gather | solution.py:154
  181.7 16.5 %fusion.109 = (bf16[3072]{0:T(1024)(128)(2,1)S(1)}, bf16[1024,3072]{1,0:T(8,128)(2,1)S(1)}) fusion(f32[1024,3072]{1,0:T(8,128)} %fusion.100, f32[3072]{0:T(1024)S(1)} %bitcast.226, bf16[3072,768]{1,0:T(8,128)(2,1)} %all-gather.12.cloned.1.call-done, bf16[1,1024,768]{1,2,0:T(8,128)(2,1)} %copy.72, f32[1024]{0:T(1024)S(1)} %fusion.92), kind=kOutput, calls=%fused_computation.147 | convolution fusion | flops 4900254720 | bytes 25188352 | tf_op jit(solution)/shard_map/rd,fd->rf/dot_general | solution.py:185
  198.3 6.7 %fusion.108 = (bf16[768]{0:T(1024)(128)(2,1)S(1)}, f32[1024,768]{1,0:T(8,128)}) fusion(bf16[1024,3072]{1,0:T(8,128)(2,1)S(1)} %get-tuple-element.338, bf16[768,3072]{1,0:T(8,128)(2,1)S(1)} %copy-done.12), kind=kOutput, calls=%fused_computation.146 | convolution fusion | flops 4832623616 | bytes 14157312 | tf_op jit(solution)/shard_map/rf,df->rd/dot_general | solution.py:189
  217.8 4.8 convolution_convert_fusion.3
  222.6 4.3 copy.74
  226.9 171.0 %while.31 = (s32[]{:T(128)}, f32[12,1,1024,64]{2,3,1,0:T(8,128)}, bf16[12,1,1024,64]{2,3,1,0:T(8,128)(2,1)}, bf16[12,1,1024,64]{2,3,1,0:T(8,128)(2,1)}, bf16[12,...) while((s32[]{:T(128)}, f32[12,1,1024,64]{2,3,1,0:T(8,128)}, ...), condition=%wide.region_12.13_spmd.clone.clone, body=%wide.region_10.12_spmd.clone.sunk.clone | while | flops 684719104 | bytes 46689448 | solution.py:247
  228.6 3.8 multiply_reduce_fusion.8
  242.9 3.8 multiply_reduce_fusion.8
  401.5 7.3 %convolution_convert_fusion.2 = bf16[768,2304]{1,0:T(8,128)(2,1)} fusion(bf16[1024,768]{0,1:T(8,128)(2,1)} %bitcast.24, bf16[1024,768]{0,1:T(8,128)(2,1)S(1)} %bitcast.214, bf16[1024,768]{0,1:T(8,128)(2,1)S(1)} %bitcast.221, bf16[1,1024,768]{1,2,0:T(8,128)(2,1)S(1)} %copy-done.1, f32[768]{0:T(1024)S(1)} %copy-done.24, f32[768]{0:T(1024)S(1)} %copy-done.19, ...), kind=kOutput, calls=%fused_computation.77 | convolution fusion | flops 3644522496 | bytes 9844736 | tf_op jit(solution)/shard_map/rd,re->de/dot_general | solution.py:255
  408.8 9.7 %convolution_convert_fusion.1 = bf16[768,3072]{1,0:T(8,128)(2,1)} fusion(bf16[1024,3072]{1,0:T(8,128)(2,1)} %copy-done.35, f32[1024,768]{0,1:T(8,128)S(1)} %get-tuple-element.332, f32[768]{0:T(1024)S(1)} %convert_element_type.246, f32[768]{0:T(1024)S(1)} %convert_element_type.245, f32[1024]{0:T(1024)S(1)} %add_rsqrt_fusion, ...), kind=kOutput, calls=%fused_computation.76 | convolution fusion | flops 4838129664 | bytes 14170112 | tf_op jit(solution)/shard_map/rd,rf->df/dot_general | solution.py:187
  418.6 13.9 %convolution_convert_fusion = bf16[3072,768]{1,0:T(8,128)(2,1)} fusion(bf16[1,1024,768]{1,2,0:T(8,128)(2,1)} %copy.72, f32[1024]{0:T(1024)S(1)} %fusion.92, f32[1024,3072]{1,0:T(8,128)} %fusion.100, f32[3072]{0:T(1024)S(1)} %bitcast.227), kind=kOutput, calls=%fused_computation.75 | convolution fusion | flops 4868014080 | bytes 18890752 | tf_op jit(solution)/shard_map/rf,rd->fd/dot_general | solution.py:183
  434.1 9.1 %fusion.107 = (bf16[768]{0:T(1024)(128)(2,1)S(1)}, f32[1024,768]{1,0:T(8,128)}) fusion(bf16[768,2304]{1,0:T(8,128)(2,1)} %all-gather.6.cloned.1.call-done, bf16[1024,768]{0,1:T(8,128)(2,1)} %bitcast.24, bf16[1024,768]{0,1:T(8,128)(2,1)} %bitcast.213, bf16[1024,768]{0,1:T(8,128)(2,1)} %bitcast.222), kind=kOutput, calls=%fused_computation.145 | convolution fusion | flops 3638820096 | bytes 11404800 | tf_op jit(solution)/shard_map/re,de->rd/dot_general | solution.py:260
  452.1 28.3 %all-reduce.17 = (bf16[768]{0:T(1024)(128)(2,1)S(1)}, bf16[768]{0:T(1024)(128)(2,1)S(1)}, bf16[768]{0:T(1024)(128)(2,1)S(1)}, bf16[768]{0:T(1024)(128)(2,1)S(1)}...) all-reduce(bf16[768]{0:T(1024)(128)(2,1)S(1)} %dynamic-update-slice, ...), channel_id=1, replica_groups=mesh['dp'=4,'fsdp'=8] {'fsdp'}, use_global_device_ids=true, to_apply=%add.7 | all-reduce | flops 9984 | bytes 39936
  481.1 10.0 %all-reduce.19 = (bf16[96]{0:T(256)(128)(2,1)S(1)}, bf16[96]{0:T(256)(128)(2,1)S(1)}, bf16[96]{0:T(256)(128)(2,1)S(1)}, bf16[96]{0:T(256)(128)(2,1)S(1)}, bf16[9...) all-reduce(bf16[96]{0:T(256)(128)(2,1)S(1)} %dynamic-slice.9, ...), channel_id=1, replica_groups=mesh['dp'=4,'fsdp'=8] {'dp'}, use_global_device_ids=true, to_apply=%region_17.18 | all-reduce | flops 1152 | bytes 4608 | tf_op jit(solution)/shard_map/psum | solution.py:293
  495.7 6.0 fusion.78
  507.6 55.4 %reduce-scatter.11.cloned.1.call-done = bf16[384,768]{1,0:T(8,128)(2,1)} async-done(((bf16[3072,768]{1,0:T(8,128)(2,1)}), bf16[384,768]{1,0:T(8,128)(2,1)}) %reduce-scatter.11.cloned.1.call-update) | async-done | bytes 589840 | tf_op jit(solution)/shard_map/reduce_scatter | solution.py:210
  562.9 11.6 %fusion.88 = bf16[1,1024,768]{1,2,0:T(8,128)(2,1)} fusion(f32[1024,768]{0,1:T(8,128)S(1)} %get-tuple-element.332, f32[768]{0:T(1024)S(1)} %convert_element_type.250, bf16[3072,768]{1,0:T(8,128)(2,1)} %all-gather.12.cloned.1.call-done, f32[1024,3072]{1,0:T(8,128)} %fusion.100, f32[3072]{0:T(1024)S(1)} %bitcast.228), kind=kOutput, calls=%fused_computation.120 | convolution fusion | flops 4865654784 | bytes 22035456 | tf_op jit(solution)/shard_map/dot_general | solution.py:167
  577.1 51.9 %all-reduce.23.cloned.1.call-done = (bf16[96,2304]{1,0:T(8,128)(2,1)}, bf16[96,768]{1,0:T(8,128)(2,1)}, bf16[96,3072]{1,0:T(8,128)(2,1)}, bf16[384,768]{1,0:T(8,128)(2,1)}) async-done(((bf16[96,2304]{1,0:T(8,128)(2,1)}, bf16[96,768]{1,0:T(8,128)(2,1)}, bf16[96,3072]{1,0:T(8,128)(2,1)}, bf16[384,768]{1,0:T(8,128)(2,1)}), (bf16[96,2304]{1,0:T(8,128)(2,1)}, bf16[96,768]{1,0:T(8,128)(2,1)}, ...) | async-done | bytes 1769488 | tf_op jit(solution)/shard_map/psum | solution.py:295
  (370 shorter events, 305.7 us)
Async XLA Ops:
  7.2 58.5 %all-gather.6.cloned.1.call-start = ((), (), s32[]{:S(2)}) async-start(), calls=%async_computation.4 | async-start | bytes 3981312 | tf_op jit(solution)/shard_map/all_gather | solution.py:120
  7.9 148.7 %all-gather.8.cloned.1.call-start = ((), (), s32[]{:S(2)}) async-start(), calls=%async_computation.5 | async-start | bytes 1327104 | tf_op jit(solution)/shard_map/all_gather | solution.py:123
  8.7 153.3 %all-gather.10.cloned.1.call-start = ((), (), s32[]{:S(2)}) async-start(), calls=%async_computation.6 | async-start | bytes 5308416 | tf_op jit(solution)/shard_map/all_gather | solution.py:152
  9.4 172.3 %all-gather.12.cloned.1.call-start = ((), (), s32[]{:S(2)}) async-start(), calls=%async_computation.7 | async-start | bytes 5308416 | tf_op jit(solution)/shard_map/all_gather | solution.py:154
  10.0 495.4 %reduce-scatter.7.cloned.1.call-start = ((), (), s32[]{:S(2)}) async-start(), calls=%async_computation.9 | async-start | bytes 1327104 | tf_op jit(solution)/shard_map/reduce_scatter | solution.py:284
  10.2 61.7 %copy-start.3 = (bf16[12,1,1024,64]{2,3,1,0:T(8,128)(2,1)}, bf16[12,1,1024,64]{2,3,1,0:T(8,128)(2,1)S(1)}, u32[]{:S(2)}) copy-start(bf16[12,1,1024,64]{2,3,1,0:T(8,128)(2,1)S(1)} %fusion.104) | copy-start | bytes 4718596
  10.3 3.6 copy-start.32
  10.3 3.9 copy-start.33
  46.9 18.7 %copy-start.18 = (f32[768]{0:T(1024)}, f32[768]{0:T(1024)S(1)}, u32[]{:S(2)}) copy-start(f32[768]{0:T(1024)S(1)} %convert_element_type.234) | copy-start | bytes 9220
  46.9 18.8 %copy-start.23 = (f32[768]{0:T(1024)}, f32[768]{0:T(1024)S(1)}, u32[]{:S(2)}) copy-start(f32[768]{0:T(1024)S(1)} %convert_element_type.235) | copy-start | bytes 9220
  48.6 17.0 %copy-start = (bf16[1,1024,768]{1,2,0:T(8,128)(2,1)}, bf16[1,1024,768]{1,2,0:T(8,128)(2,1)S(1)}, u32[]{:S(2)}) copy-start(bf16[1,1024,768]{1,2,0:T(8,128)(2,1)S(1)} %copy.64) | copy-start | bytes 4718596
  48.6 4.2 copy-start.26
  48.9 23.0 %copy-start.16 = (f32[1024]{0:T(1024)}, f32[1024]{0:T(1024)S(1)}, u32[]{:S(2)}) copy-start(f32[1024]{0:T(1024)S(1)} %broadcast_multiply_fusion.5) | copy-start | bytes 12292
  49.4 22.6 %copy-start.20 = (f32[1024]{0:T(1024)}, f32[1024]{0:T(1024)S(1)}, u32[]{:S(2)}) copy-start(f32[1024]{0:T(1024)S(1)} %add_rsqrt_fusion.1) | copy-start | bytes 12292
  181.7 16.5 %copy-start.12 = (bf16[768,3072]{1,0:T(8,128)(2,1)S(1)}, bf16[768,3072]{1,0:T(8,128)(2,1)}, u32[]{:S(2)}) copy-start(bf16[768,3072]{1,0:T(8,128)(2,1)} %all-gather.10.cloned.1.call-done) | copy-start | bytes 14155780
  198.3 6.8 %copy-start.35 = (bf16[1024,3072]{1,0:T(8,128)(2,1)}, bf16[1024,3072]{1,0:T(8,128)(2,1)S(1)}, u32[]{:S(2)}) copy-start(bf16[1024,3072]{1,0:T(8,128)(2,1)S(1)} %get-tuple-element.338) | copy-start | bytes 18874372
  217.7 287.6 %reduce-scatter.5.cloned.1.call-start = ((), (), s32[]{:S(2)}) async-start(), calls=%async_computation.8 | async-start | bytes 3981312 | tf_op jit(solution)/shard_map/reduce_scatter | solution.py:275
  397.8 3.6 copy-start.17
  397.8 3.6 copy-start.19
  408.8 98.8 %reduce-scatter.9.cloned.1.call-start = ((), (), s32[]{:S(2)}) async-start(), calls=%async_computation.10 | async-start | bytes 5308416 | tf_op jit(solution)/shard_map/reduce_scatter | solution.py:204
  418.6 144.3 %reduce-scatter.11.cloned.1.call-start = ((), (), s32[]{:S(2)}) async-start(), calls=%async_computation.11 | async-start | bytes 5308416 | tf_op jit(solution)/shard_map/reduce_scatter | solution.py:210
  432.5 196.5 %all-reduce.23.cloned.1.call-start = ((), (), s32[]{:S(2)}) async-start(), calls=%async_computation.12 | async-start | bytes 3538944 | tf_op jit(solution)/shard_map/psum | solution.py:295
  629.0 4.4 copy-start.14
  629.0 5.4 copy-start.15
  (43 other events, 93.2 us)
Sparse Core Ops, SparseCore 0:
  9.6 44.6 all-gather.5
  56.0 21.6 all-gather.7
  79.3 50.8 all-gather.9
  131.7 49.9 all-gather.11
  217.8 31.6 reduce-scatter.6
  408.9 42.4 reduce-scatter.4
  453.7 53.8 reduce-scatter.8
  509.9 53.0 reduce-scatter.10
  566.4 62.6 all-reduce.22
where the time goes:
time: 652 us; the launch traced here: 642 us
  matrix products  307 us (47%)
  waiting for transfers between devices  121 us (19%)
  blocking collectives  83.5 us (13%)
  local copies, waits for them, and re-layouts  57.5 us (9%)
  other arithmetic  54 us (8%)
  between operations  17.4 us (3%)
    unnamed x2, blocking collectives  60.8 us
    reduce_scatter x1, waiting for transfers between devices, per_device(): lax.psum_scatter(grad_down.astype(jnp.bfloat16), 'fsdp', scatter_dimensio...  55.4 us
    psum x1, waiting for transfers between devices, per_device(): lax.psum(row_qkv.astype(jnp.bfloat16), 'dp').astype(jnp.float32)  51.9 us
    dot_general x12, matrix products, head_backward(): jnp.einsum('sqd,skd->sqk', query_head, key_head, preferred_element_type=j...  45.3 us
    dot_general x12, matrix products, head_forward(): jnp.einsum('sqd,skd->sqk', query_head, key_head, preferred_element_type=j...  39.4 us
    dot_general x12, matrix products, head_backward(): jnp.einsum('sqk,sqd->skd', softmax_rows.astype(jnp.bfloat16), grad_head,...  28.5 us
    dot_general x12, matrix products, head_backward(): jnp.einsum('sqk,skd->sqd', grad_scores, key_head, preferred_element_type=...  27.8 us
    unnamed x103, local copies, waits for them, and re-layouts  27.4 us
  transfers between devices with their start and end apart: 9, of which 4 were waited for; matrix products, arithmetic and copies ran while one was open for 56% of the time, Pallas kernels for 0%

commit v1 on v0

--- a/solution.py
+++ b/solution.py
@@ -4,6 +4,7 @@
 import jax.numpy as jnp
 from jax import lax
 from jax.sharding import PartitionSpec as P
+from jax.lax import all_gather
 
 H = 12
 EPSILON = 1e-05
@@ -292,7 +293,7 @@
     attn_sums = (
         lax.psum(row_gain_one.astype(jnp.bfloat16), "dp").astype(jnp.float32),
         lax.psum(row_shift_one.astype(jnp.bfloat16), "dp").astype(jnp.float32),
-        lax.psum(row_qkv.astype(jnp.bfloat16), "dp").astype(jnp.float32),
+        jnp.sum(all_gather(row_qkv.astype(jnp.bfloat16), axis_name="dp"), 0).astype(jnp.float32),
         lax.psum(row_query.astype(jnp.bfloat16), "dp").astype(jnp.float32),
         lax.psum(row_value.astype(jnp.bfloat16), "dp").astype(jnp.float32),
         lax.psum(row_out.astype(jnp.bfloat16), "dp").astype(jnp.float32),

time: 652 us -> 706 us (1.083)
  waiting for transfers between devices: 121 us -> 179 us
    reduce_scatter x1, waiting for transfers between devices: 2.21 us -> 43.2 us  [per_device(): lax.psum_scatter(grad_up.astype(jnp.bfloat16), 'fsdp', scatter_dimension=...]
    reduce_scatter x1, waiting for transfers between devices: 0.01 us -> 14.1 us  [per_device(): lax.psum_scatter(grad_qkv.astype(jnp.bfloat16), 'fsdp', scatter_dimension...]
    unnamed x103 -> x101, local copies, waits for them, and re-layouts: 27.4 us -> 24.7 us
  transfers between devices with their start and end apart: 9 -> 10, of which waited for: 4 -> 5; matrix products, arithmetic and copies ran while one was open for 56% -> 27% of each run, Pallas kernels for 0% -> 0%
where the time goes in v1:
time: 706 us; the launch traced here: 696 us
  matrix products  307 us (43%)
  waiting for transfers between devices  179 us (25%)
  blocking collectives  82.4 us (12%)
  local copies, waits for them, and re-layouts  54.7 us (8%)
  other arithmetic  53.9 us (8%)
  between operations  17.9 us (3%)
    unnamed x2, blocking collectives  59.4 us
    reduce_scatter x1, waiting for transfers between devices, per_device(): lax.psum_scatter(grad_down.astype(jnp.bfloat16), 'fsdp', scatter_dimensio...  55.4 us
    psum x1, waiting for transfers between devices, per_device(): lax.psum(row_out.astype(jnp.bfloat16), 'dp').astype(jnp.float32)  54.1 us
    dot_general x12, matrix products, head_backward(): jnp.einsum('sqd,skd->sqk', query_head, key_head, preferred_element_type=j...  45.3 us
    reduce_scatter x1, waiting for transfers between devices, per_device(): lax.psum_scatter(grad_up.astype(jnp.bfloat16), 'fsdp', scatter_dimension=...  43.2 us
    dot_general x12, matrix products, head_forward(): jnp.einsum('sqd,skd->sqk', query_head, key_head, preferred_element_type=j...  39.5 us
    dot_general x12, matrix products, head_backward(): jnp.einsum('sqk,sqd->skd', softmax_rows.astype(jnp.bfloat16), grad_head,...  28.5 us
    dot_general x12, matrix products, head_backward(): jnp.einsum('sqk,skd->sqd', grad_scores, key_head, preferred_element_type=...  27.8 us
  transfers between devices with their start and end apart: 10, of which 5 were waited for; matrix products, arithmetic and copies ran while one was open for 27% of the time, Pallas kernels for 0%

profile of v1, /device:TPU:0, one launch (start us, length us, event | category | flops | bytes accessed | tf_op | source)
XLA Modules:
  0.0 696.0 jit_solution(16230542805820119457)
XLA Ops:
  14.4 32.5 %all-reduce.18 = (bf16[768]{0:T(1024)(128)(2,1)S(1)}, bf16[768]{0:T(1024)(128)(2,1)S(1)}, bf16[768]{0:T(1024)(128)(2,1)S(1)}, bf16[768]{0:T(1024)(128)(2,1)S(1)}...) all-reduce(bf16[768]{0:T(1024)(128)(2,1)S(1)} %dynamic-update-slice, ...), channel_id=1, replica_groups=mesh['dp'=4,'fsdp'=8] {'fsdp'}, use_global_device_ids=true, to_apply=%add.1 | all-reduce | flops 5376 | bytes 21504
  52.8 12.7 %all-gather.1 = bf16[8,1,384]{2,1,0:T(2,128)(2,1)S(1)} all-gather(bf16[1,1,384]{2,1,0:T(2,128)(2,1)S(1)} %reshape.387), channel_id=1, replica_groups=mesh['dp'=4,'fsdp'=8] {'fsdp'}, dimensions={0}, use_global_device_ids=true | all-gather | bytes 6912 | tf_op jit(solution)/shard_map/all_gather | solution.py:154
  65.6 6.3 fusion.98
  87.1 69.5 %while.30 = (s32[]{:T(128)}, bf16[12,1,1024,64]{2,3,1,0:T(8,128)(2,1)S(1)}, f32[12,1,1024]{2,1,0:T(1,128)S(1)}, bf16[12,1,1024,64]{3,2,1,0:T(8,128)(2,1)}, bf16[...) while((s32[]{:T(128)}, ...), condition=%wide.region_5.6_spmd.clone.clone, body=%wide.region_2.5_spmd.clone.sunk.clone | while | flops 281017344 | bytes 13676633 | solution.py:141
  157.7 3.9 fusion.106
  162.0 10.7 %fusion.100 = f32[1024,3072]{1,0:T(8,128)} fusion(bf16[768,3072]{1,0:T(8,128)(2,1)} %all-gather.12.cloned.1.call-done, f32[1024,768]{0,1:T(8,128)S(1)} %get-tuple-element.331, f32[768]{0:T(1024)S(1)} %convert_element_type.248, f32[768]{0:T(1024)S(1)} %convert_element_type.247, f32[1024]{0:T(1024)S(1)} %add_rsqrt_fusion, f32[1024]{0:T(1024)S(1)} %broadcast_multiply_fusion.4), kind=kOutput, calls=%fused_computation.139 | convolution fusion | flops 4835770368 | bytes 20461568 | tf_op jit(solution)/shard_map/dot_general | solution.py:163
  172.7 9.0 %all-gather.14.cloned.1.call-done = bf16[3072,768]{1,0:T(8,128)(2,1)} async-done(((bf16[384,768]{1,0:T(8,128)(2,1)}), bf16[3072,768]{1,0:T(8,128)(2,1)}) %all-gather.14.cloned.1.call-update) | async-done | bytes 4718608 | tf_op jit(solution)/shard_map/all_gather | solution.py:155
  181.7 16.5 %fusion.109 = (bf16[3072]{0:T(1024)(128)(2,1)S(1)}, bf16[1024,3072]{1,0:T(8,128)(2,1)S(1)}) fusion(f32[1024,3072]{1,0:T(8,128)} %fusion.100, f32[3072]{0:T(1024)S(1)} %bitcast.228, bf16[3072,768]{1,0:T(8,128)(2,1)} %all-gather.14.cloned.1.call-done, bf16[1,1024,768]{1,2,0:T(8,128)(2,1)} %copy.72, f32[1024]{0:T(1024)S(1)} %fusion.92), kind=kOutput, calls=%fused_computation.147 | convolution fusion | flops 4900254720 | bytes 25188352 | tf_op jit(solution)/shard_map/rd,fd->rf/dot_general | solution.py:186
  198.2 6.8 fusion.108
  216.3 4.1 copy.74
  220.4 171.1 %while.31 = (s32[]{:T(128)}, f32[12,1,1024,64]{2,3,1,0:T(8,128)}, bf16[12,1,1024,64]{2,3,1,0:T(8,128)(2,1)}, bf16[12,1,1024,64]{2,3,1,0:T(8,128)(2,1)}, bf16[12,...) while((s32[]{:T(128)}, f32[12,1,1024,64]{2,3,1,0:T(8,128)}, ...), condition=%wide.region_12.13_spmd.clone.clone, body=%wide.region_10.12_spmd.clone.sunk.clone | while | flops 684719104 | bytes 46689448 | solution.py:248
  395.2 7.3 %convolution_convert_fusion.2 = bf16[768,2304]{1,0:T(8,128)(2,1)} fusion(bf16[1024,768]{0,1:T(8,128)(2,1)} %bitcast.24, bf16[1024,768]{0,1:T(8,128)(2,1)S(1)} %bitcast.215, bf16[1024,768]{0,1:T(8,128)(2,1)S(1)} %bitcast.223, bf16[1,1024,768]{1,2,0:T(8,128)(2,1)S(1)} %copy-done.1, f32[768]{0:T(1024)S(1)} %copy-done.22, f32[768]{0:T(1024)S(1)} %copy-done.17, ...), kind=kOutput, calls=%fused_computation.77 | convolution fusion | flops 3644522496 | bytes 9844736 | tf_op jit(solution)/shard_map/rd,re->de/dot_general | solution.py:256
  402.6 4.8 convolution_convert_fusion.4
  407.4 9.8 %convolution_convert_fusion.1 = bf16[768,3072]{1,0:T(8,128)(2,1)} fusion(bf16[1024,3072]{1,0:T(8,128)(2,1)} %copy-done.34, f32[1024,768]{0,1:T(8,128)S(1)} %get-tuple-element.331, f32[768]{0:T(1024)S(1)} %convert_element_type.248, f32[768]{0:T(1024)S(1)} %convert_element_type.247, f32[1024]{0:T(1024)S(1)} %add_rsqrt_fusion, ...), kind=kOutput, calls=%fused_computation.76 | convolution fusion | flops 4838129664 | bytes 14170112 | tf_op jit(solution)/shard_map/rd,rf->df/dot_general | solution.py:188
  417.3 13.7 %convolution_convert_fusion = bf16[3072,768]{1,0:T(8,128)(2,1)} fusion(bf16[1,1024,768]{1,2,0:T(8,128)(2,1)} %copy.72, f32[1024]{0:T(1024)S(1)} %fusion.92, f32[1024,3072]{1,0:T(8,128)} %fusion.100, f32[3072]{0:T(1024)S(1)} %bitcast.229), kind=kOutput, calls=%fused_computation.75 | convolution fusion | flops 4868014080 | bytes 18890752 | tf_op jit(solution)/shard_map/rf,rd->fd/dot_general | solution.py:184
  431.0 14.1 %reduce-scatter.5.cloned.1.call-done = bf16[96,2304]{1,0:T(8,128)(2,1)} async-done(((bf16[768,2304]{1,0:T(8,128)(2,1)}), bf16[96,2304]{1,0:T(8,128)(2,1)}) %reduce-scatter.5.cloned.1.call-update) | async-done | bytes 442384 | tf_op jit(solution)/shard_map/reduce_scatter | solution.py:276
  447.0 9.0 %fusion.107 = (bf16[768]{0:T(1024)(128)(2,1)S(1)}, f32[1024,768]{1,0:T(8,128)}) fusion(bf16[768,2304]{1,0:T(8,128)(2,1)} %all-gather.8.cloned.1.call-done, bf16[1024,768]{0,1:T(8,128)(2,1)} %bitcast.24, bf16[1024,768]{0,1:T(8,128)(2,1)} %bitcast.214, bf16[1024,768]{0,1:T(8,128)(2,1)} %bitcast.224), kind=kOutput, calls=%fused_computation.145 | convolution fusion | flops 3638820096 | bytes 11404800 | tf_op jit(solution)/shard_map/re,de->rd/dot_general | solution.py:261
  464.8 26.9 %all-reduce.17 = (bf16[768]{0:T(1024)(128)(2,1)S(1)}, bf16[768]{0:T(1024)(128)(2,1)S(1)}, bf16[768]{0:T(1024)(128)(2,1)S(1)}, bf16[768]{0:T(1024)(128)(2,1)S(1)}...) all-reduce(bf16[768]{0:T(1024)(128)(2,1)S(1)} %dynamic-update-slice, ...), channel_id=1, replica_groups=mesh['dp'=4,'fsdp'=8] {'fsdp'}, use_global_device_ids=true, to_apply=%add.7 | all-reduce | flops 9984 | bytes 39936
  491.7 43.2 %reduce-scatter.9.cloned.1.call-done = bf16[96,3072]{1,0:T(8,128)(2,1)} async-done(((bf16[768,3072]{1,0:T(8,128)(2,1)}), bf16[96,3072]{1,0:T(8,128)(2,1)}) %reduce-scatter.9.cloned.1.call-update) | async-done | bytes 589840 | tf_op jit(solution)/shard_map/reduce_scatter | solution.py:205
  534.9 55.4 %reduce-scatter.11.cloned.1.call-done = bf16[384,768]{1,0:T(8,128)(2,1)} async-done(((bf16[3072,768]{1,0:T(8,128)(2,1)}), bf16[384,768]{1,0:T(8,128)(2,1)}) %reduce-scatter.11.cloned.1.call-update) | async-done | bytes 589840 | tf_op jit(solution)/shard_map/reduce_scatter | solution.py:211
  590.3 11.6 %fusion.88 = bf16[1,1024,768]{1,2,0:T(8,128)(2,1)} fusion(f32[1024,768]{0,1:T(8,128)S(1)} %get-tuple-element.331, f32[768]{0:T(1024)S(1)} %convert_element_type.252, bf16[3072,768]{1,0:T(8,128)(2,1)} %all-gather.14.cloned.1.call-done, f32[1024,3072]{1,0:T(8,128)} %fusion.100, f32[3072]{0:T(1024)S(1)} %bitcast.230), kind=kOutput, calls=%fused_computation.120 | convolution fusion | flops 4865654784 | bytes 22035456 | tf_op jit(solution)/shard_map/dot_general | solution.py:168
  602.5 10.2 %all-reduce.19 = (bf16[96]{0:T(256)(128)(2,1)S(1)}, bf16[96]{0:T(256)(128)(2,1)S(1)}, bf16[96]{0:T(256)(128)(2,1)S(1)}, bf16[96]{0:T(256)(128)(2,1)S(1)}, bf16[9...) all-reduce(bf16[96]{0:T(256)(128)(2,1)S(1)} %dynamic-slice.9, ...), channel_id=1, replica_groups=mesh['dp'=4,'fsdp'=8] {'dp'}, use_global_device_ids=true, to_apply=%region_17.18 | all-reduce | flops 1152 | bytes 4608 | tf_op jit(solution)/shard_map/psum | solution.py:294
  617.5 4.3 fusion.78
  629.4 54.1 %all-reduce.23.cloned.1.call-done = (bf16[96,768]{1,0:T(8,128)(2,1)}, bf16[96,3072]{1,0:T(8,128)(2,1)}, bf16[384,768]{1,0:T(8,128)(2,1)}) async-done(((bf16[96,768]{1,0:T(8,128)(2,1)}, bf16[96,3072]{1,0:T(8,128)(2,1)}, bf16[384,768]{1,0:T(8,128)(2,1)}), (bf16[96,768]{1,0:T(8,128)(2,1)}, bf16[96,3072]{1,0:T(8,128)(2,1)}, bf16[384,768]{1,0:T(8,128)(2,1)})) %all-reduce.23.cloned.1.call-update) | async-done | bytes 1327120 | tf_op jit(solution)/shard_map/psum | solution.py:299
  (372 shorter events, 310.3 us)
Async XLA Ops:
  7.2 58.4 %all-gather.8.cloned.1.call-start = ((), (), s32[]{:S(2)}) async-start(), calls=%async_computation.4 | async-start | bytes 3981312 | tf_op jit(solution)/shard_map/all_gather | solution.py:121
  7.9 148.7 %all-gather.10.cloned.1.call-start = ((), (), s32[]{:S(2)}) async-start(), calls=%async_computation.5 | async-start | bytes 1327104 | tf_op jit(solution)/shard_map/all_gather | solution.py:124
  8.7 153.3 %all-gather.12.cloned.1.call-start = ((), (), s32[]{:S(2)}) async-start(), calls=%async_computation.6 | async-start | bytes 5308416 | tf_op jit(solution)/shard_map/all_gather | solution.py:153
  9.4 172.3 %all-gather.14.cloned.1.call-start = ((), (), s32[]{:S(2)}) async-start(), calls=%async_computation.7 | async-start | bytes 5308416 | tf_op jit(solution)/shard_map/all_gather | solution.py:155
  10.0 435.2 %reduce-scatter.5.cloned.1.call-start = ((), (), s32[]{:S(2)}) async-start(), calls=%async_computation.8 | async-start | bytes 3981312 | tf_op jit(solution)/shard_map/reduce_scatter | solution.py:276
  10.2 61.7 %copy-start.3 = (bf16[12,1,1024,64]{2,3,1,0:T(8,128)(2,1)}, bf16[12,1,1024,64]{2,3,1,0:T(8,128)(2,1)S(1)}, u32[]{:S(2)}) copy-start(bf16[12,1,1024,64]{2,3,1,0:T(8,128)(2,1)S(1)} %fusion.104) | copy-start | bytes 4718596
  10.3 3.6 copy-start.31
  10.3 3.8 copy-start.32
  46.9 18.7 %copy-start.16 = (f32[768]{0:T(1024)}, f32[768]{0:T(1024)S(1)}, u32[]{:S(2)}) copy-start(f32[768]{0:T(1024)S(1)} %convert_element_type.236) | copy-start | bytes 9220
  46.9 18.7 %copy-start.21 = (f32[768]{0:T(1024)}, f32[768]{0:T(1024)S(1)}, u32[]{:S(2)}) copy-start(f32[768]{0:T(1024)S(1)} %convert_element_type.237) | copy-start | bytes 9220
  48.6 17.0 %copy-start = (bf16[1,1024,768]{1,2,0:T(8,128)(2,1)}, bf16[1,1024,768]{1,2,0:T(8,128)(2,1)S(1)}, u32[]{:S(2)}) copy-start(bf16[1,1024,768]{1,2,0:T(8,128)(2,1)S(1)} %copy.64) | copy-start | bytes 4718596
  48.6 4.1 copy-start.24
  48.9 23.0 %copy-start.14 = (f32[1024]{0:T(1024)}, f32[1024]{0:T(1024)S(1)}, u32[]{:S(2)}) copy-start(f32[1024]{0:T(1024)S(1)} %broadcast_multiply_fusion.5) | copy-start | bytes 12292
  49.4 22.5 %copy-start.18 = (f32[1024]{0:T(1024)}, f32[1024]{0:T(1024)S(1)}, u32[]{:S(2)}) copy-start(f32[1024]{0:T(1024)S(1)} %add_rsqrt_fusion.1) | copy-start | bytes 12292
  181.7 16.5 %copy-start.11 = (bf16[768,3072]{1,0:T(8,128)(2,1)S(1)}, bf16[768,3072]{1,0:T(8,128)(2,1)}, u32[]{:S(2)}) copy-start(bf16[768,3072]{1,0:T(8,128)(2,1)} %all-gather.12.cloned.1.call-done) | copy-start | bytes 14155780
  198.2 6.8 copy-start.34
  391.6 3.6 copy-start.1
  402.5 89.2 %reduce-scatter.7.cloned.1.call-start = ((), (), s32[]{:S(2)}) async-start(), calls=%async_computation.9 | async-start | bytes 1327104 | tf_op jit(solution)/shard_map/reduce_scatter | solution.py:285
  407.4 127.5 %reduce-scatter.9.cloned.1.call-start = ((), (), s32[]{:S(2)}) async-start(), calls=%async_computation.10 | async-start | bytes 5308416 | tf_op jit(solution)/shard_map/reduce_scatter | solution.py:205
  417.2 173.0 %reduce-scatter.11.cloned.1.call-start = ((), (), s32[]{:S(2)}) async-start(), calls=%async_computation.11 | async-start | bytes 5308416 | tf_op jit(solution)/shard_map/reduce_scatter | solution.py:211
  430.9 15.6 %copy-start.33 = (bf16[96]{0:T(256)(128)(2,1)S(1)}, bf16[96]{0:T(256)(128)(2,1)}, u32[]{:S(2)}) copy-start(bf16[96]{0:T(256)(128)(2,1)} %param.37) | copy-start | bytes 580
  431.0 195.7 %all-gather.16.cloned.1.call-start = ((), (), s32[]{:S(2)}) async-start(), calls=%async_computation.12 | async-start | bytes 2211840 | tf_op jit(solution)/shard_map/all_gather | solution.py:296
  445.2 238.4 %all-reduce.23.cloned.1.call-start = ((), (), s32[]{:S(2)}) async-start(), calls=%async_computation.13 | async-start | bytes 2654208 | tf_op jit(solution)/shard_map/psum | solution.py:299
  683.6 4.4 copy-start.13
  (43 other events, 94.5 us)
Sparse Core Ops, SparseCore 0:
  9.6 44.6 all-gather.7
  56.0 21.6 all-gather.9
  79.3 50.8 all-gather.11
  131.7 49.9 all-gather.13
  402.6 42.4 reduce-scatter.4
  447.9 31.5 reduce-scatter.6
  481.8 53.0 reduce-scatter.8
  537.2 53.0 reduce-scatter.10
  592.1 31.0 all-gather.15
  626.4 57.0 all-reduce.22
